TPU v7x, 32 devices: a whole 2x2x4 slice. The times are simulated.
32 devices in a mesh: gx: 4 (over z), gy: 4 (over x, core), gz: 2 (over y).
Axes of the slice: x: 2, y: 2, z: 4, core: 2. Of those that a mesh axis runs over, the one named last changes fastest.
Arguments:
- krylov_basis: float32 [60, 16, 32, 256], P(None, 'gx', 'gy', 'gz'), may hold values from -6 to 6
- schur_vectors: float32 [60, 20], replicated, may hold values from -1 to 1, as said below
- next_vector: float32 [16, 32, 256], P('gx', 'gy', 'gz'), may hold values from -10 to 10
- diag_shift: float32 [16, 32, 256], P('gx', 'gy', 'gz'), may hold values from 0.25 to 2
- velocity: float32 [3, 16, 32, 256], P(None, 'gx', 'gy', 'gz'), may hold values from -1 to 1
Outputs:
- new_basis: float32 [24, 16, 32, 256], P(None, 'gx', 'gy', 'gz')
- hessenberg: float32 [24, 3], replicated
Inputs may be any that keep to these rules, and one draw needn't show every extreme that they name: `schur_vectors`: the columns are orthonormal.
All inputs are finite; a program needn't handle non-finite values.
Results may differ from a plain program's by a relative error of at most 0.0003.
Values sent between devices are 32-bit elements; how exact they have to be, the bound alone decides.
A program may use at most 64 MiB of HBM per device.

v0:
```python
import jax
import jax.numpy as jnp
from jax import lax
from jax.sharding import PartitionSpec as P

KEEP = 20
EXPAND = 3
ROWS = 24


def with_halo(value, sides, width):
    for axis, dim in sides:
        count, length = (lax.axis_size(axis), value.shape[dim])
        up = [(i, (i + 1) % count) for i in range(count - 1)]
        down = [(j, i) for i, j in up]
        last = lax.slice_in_dim(value, length - width, length, axis=dim)
        initial = lax.slice_in_dim(value, 0, width, axis=dim)
        before = lax.ppermute(last, axis, up)
        after = lax.ppermute(initial, axis, down)
        value = jnp.concatenate([before, value, after], axis=dim)
    return value


def combine_terms(
    field, x_ahead, x_behind, y_ahead, y_behind, z_ahead, z_behind, diag_shift, velocity
):
    neighbours = x_ahead + x_behind + y_ahead + y_behind + z_ahead + z_behind
    flow = (
        velocity[0] * (x_ahead - x_behind)
        + velocity[1] * (y_ahead - y_behind)
        + velocity[2] * (z_ahead - z_behind)
    )
    return (6.0 + diag_shift) * field - neighbours + 0.5 * flow


def operate_field(field, diag_shift, velocity):
    padded = with_halo(field, (("gx", 0), ("gy", 1), ("gz", 2)), 1)
    return combine_terms(
        field,
        padded[2:, 1:-1, 1:-1],
        padded[:-2, 1:-1, 1:-1],
        padded[1:-1, 2:, 1:-1],
        padded[1:-1, :-2, 1:-1],
        padded[1:-1, 1:-1, 2:],
        padded[1:-1, 1:-1, :-2],
        diag_shift,
        velocity,
    )


def per_device(krylov_basis, schur_vectors, next_vector, diag_shift, velocity):
    highest = lax.Precision.HIGHEST
    shape_local = next_vector.shape
    cell_count = (
        shape_local[0]
        * shape_local[1]
        * shape_local[2]
        * lax.axis_size("gx")
        * lax.axis_size("gy")
        * lax.axis_size("gz")
    )
    rotated = jnp.einsum("ik,ixyz->kxyz", schur_vectors, krylov_basis, precision=highest)
    columns = []
    starting = jnp.concatenate([rotated, next_vector[None]], axis=0)
    flat_start = starting.reshape(KEEP + 1, -1)
    gram_matrix = (
        lax.psum(jnp.dot(flat_start, flat_start.T, precision=highest), ("gx", "gy", "gz"))
        / cell_count
    )
    divisor = jnp.maximum(jnp.sqrt(gram_matrix[KEEP, KEEP]), 0.5)
    factor = jnp.ones((KEEP + 1,), jnp.float32).at[KEEP].set(1.0 / divisor)
    gram_matrix = gram_matrix * factor[:, None] * factor[None, :]
    vectors = jnp.concatenate([rotated, (next_vector / divisor)[None]], axis=0)
    for expansion in range(EXPAND):
        count = vectors.shape[0]
        flat_basis = vectors.reshape(count, -1)
        applied = operate_field(vectors[-1], diag_shift, velocity).reshape(-1)
        dotted, self_sum = lax.psum(
            (jnp.dot(flat_basis, applied, precision=highest), jnp.sum(applied * applied)),
            ("gx", "gy", "gz"),
        )
        first_coeffs = dotted / cell_count
        self_norm = self_sum / cell_count
        second_coeffs = first_coeffs - jnp.dot(gram_matrix, first_coeffs, precision=highest)
        total_coeffs = first_coeffs + second_coeffs
        partly = applied - jnp.dot(first_coeffs, flat_basis, precision=highest)
        cleaned = partly - jnp.dot(second_coeffs, flat_basis, precision=highest)
        length_sq = (
            self_norm
            - 2.0 * jnp.dot(total_coeffs, first_coeffs, precision=highest)
            + jnp.dot(
                total_coeffs,
                jnp.dot(gram_matrix, total_coeffs, precision=highest),
                precision=highest,
            )
        )
        length = jnp.sqrt(jnp.maximum(length_sq, 0.0))
        divisor = jnp.maximum(length, 0.5)
        column = jnp.zeros((ROWS,), jnp.float32)
        column = column.at[:count].set(total_coeffs).at[count].set(length)
        columns.append(column)
        newest = (cleaned / divisor).reshape(shape_local)
        vectors = jnp.concatenate([vectors, newest[None]], axis=0)
        intersect = (
            second_coeffs - jnp.dot(gram_matrix, second_coeffs, precision=highest)
        ) / divisor
        corner = jnp.maximum(length_sq, 0.0) / (divisor * divisor)
        upper_rows = jnp.concatenate([gram_matrix, intersect[:, None]], axis=1)
        lower_row = jnp.concatenate([intersect, corner[None]], axis=0)
        gram_matrix = jnp.concatenate([upper_rows, lower_row[None]], axis=0)
    return (vectors, jnp.stack(columns, axis=1))


def solution(mesh):
    in_specs = (
        P(None, "gx", "gy", "gz"),
        P(),
        P("gx", "gy", "gz"),
        P("gx", "gy", "gz"),
        P(None, "gx", "gy", "gz"),
    )
    out_specs = (P(None, "gx", "gy", "gz"), P())
    return jax.shard_map(
        per_device, mesh=mesh, in_specs=in_specs, out_specs=out_specs, check_vma=False
    )
```

profile of v0, /device:TPU:0, one launch (start us, length us, event | category | flops | bytes accessed | tf_op | source)
XLA Modules:
  0.0 258.3 jit_solution(9260418553971904028)
XLA Ops:
  0.7 1.2 copy-done
  1.8 1.9 fusion.10
  3.7 0.5 convolution_bitcast_fusion
  4.2 42.1 %psum.49 = f32[21,21]{1,0:T(8,128)S(1)} all-reduce(f32[21,21]{1,0:T(8,128)S(1)} %convolution_bitcast_fusion), channel_id=1, replica_groups=mesh['gx'=4,'gy'=4,'gz'=2] {'gx','gy','gz'}, use_global_device_ids=true, to_apply=%region_0.0 | all-reduce | flops 441 | bytes 3528 | tf_op jit(solution)/shard_map/psum | solution.py:67
  46.3 0.6 slice.304
  47.6 1.3 collective-permute-start
  48.9 4.5 %collective-permute-start.1 = (f32[1,8,128]{2,1,0:T(8,128)S(1)}, f32[1,8,128]{2,1,0:T(8,128)S(1)}, u32[]{:S(2)}, u32[]{:S(2)}) collective-permute-start(f32[1,8,128]{2,1,0:T(8,128)S(1)} %get-tuple-element.124), channel_id=1, source_target_pairs={{0,8},{8,16},{16,24},{1,9},{9,17},{17,25},{2,10},{10,18},{18,26},{... | collective-permute-start | bytes 12296 | tf_op jit(solution)/shard_map/ppermute | solution.py:18
  53.7 1.1 collective-permute-done.1
  54.8 1.3 collective-permute-start.2
  56.1 3.0 %collective-permute-start.3 = (f32[6,1,128]{2,1,0:T(1,128)S(1)}, f32[6,1,128]{2,1,0:T(1,128)S(1)}, u32[]{:S(2)}, u32[]{:S(2)}) collective-permute-start(f32[6,1,128]{2,1,0:T(1,128)S(1)} %get-tuple-element.118), channel_id=1, source_target_pairs={{0,2},{2,4},{4,6},{1,3},{3,5},{5,7},{8,10},{10,12},{12,14},{9,11},... | collective-permute-start | bytes 9224 | tf_op jit(solution)/shard_map/ppermute | solution.py:18
  59.3 0.7 collective-permute-done.3
  60.0 4.2 %collective-permute-start.5 = (f32[6,10,1]{2,1,0:T(8,128)S(1)}, f32[6,10,1]{2,1,0:T(8,128)S(1)}, u32[]{:S(2)}, u32[]{:S(2)}) collective-permute-start(f32[6,10,1]{2,1,0:T(8,128)S(1)} %get-tuple-element.113), channel_id=1, source_target_pairs={{0,1},{2,3},{4,5},{6,7},{8,9},{10,11},{12,13},{14,15},{16,17},{18,... | collective-permute-start | bytes 728 | tf_op jit(solution)/shard_map/ppermute | solution.py:18
  64.2 1.3 collective-permute-start.4
  65.6 0.2 copy.36
  65.8 0.1 collective-permute-done.5
  66.0 4.3 %collective-permute-done.4 = f32[6,10,1]{2,1,0:T(8,128)S(1)} collective-permute-done((f32[6,10,1]{2,1,0:T(8,128)S(1)}, f32[6,10,1]{2,1,0:T(8,128)S(1)}, u32[]{:S(2)}, u32[]{:S(2)}) %collective-permute-start.4) | collective-permute-done | bytes 272 | tf_op jit(solution)/shard_map/ppermute | solution.py:19
  70.2 0.7 multiply_reduce_fusion.2
  70.9 0.5 convolution_bitcast_fusion.11
  71.4 40.6 %all-reduce.6 = (f32[21]{0:T(128)S(1)}, f32[]{:T(128)}) all-reduce(f32[21]{0:T(128)S(1)} %convolution_bitcast_fusion.11, f32[]{:T(128)} %get-tuple-element.106), channel_id=1, replica_groups=mesh['gx'=4,'gy'=4,'gz'=2] {'gx','gy','gz'}, use_global_device_ids=true, to_apply=%region_1.0 | all-reduce | flops 22 | bytes 176 | tf_op jit(solution)/shard_map/psum | solution.py:78
  112.0 0.7 multiply_reduce_fusion.5
  112.7 0.3 fusion.34
  113.1 0.3 fusion.33
  114.1 0.7 fusion.12
  116.2 0.1 fusion.8
  116.3 1.3 collective-permute-start.6
  117.6 4.5 %collective-permute-start.7 = (f32[1,8,128]{2,1,0:T(8,128)S(1)}, f32[1,8,128]{2,1,0:T(8,128)S(1)}, u32[]{:S(2)}, u32[]{:S(2)}) collective-permute-start(f32[1,8,128]{2,1,0:T(8,128)S(1)} %get-tuple-element.122), channel_id=1, source_target_pairs={{0,8},{8,16},{16,24},{1,9},{9,17},{17,25},{2,10},{10,18},{18,26},{... | collective-permute-start | bytes 12296 | tf_op jit(solution)/shard_map/ppermute | solution.py:18
  122.5 1.0 collective-permute-done.7
  123.5 1.3 collective-permute-start.8
  124.8 3.0 %collective-permute-start.9 = (f32[6,1,128]{2,1,0:T(1,128)S(1)}, f32[6,1,128]{2,1,0:T(1,128)S(1)}, u32[]{:S(2)}, u32[]{:S(2)}) collective-permute-start(f32[6,1,128]{2,1,0:T(1,128)S(1)} %get-tuple-element.116), channel_id=1, source_target_pairs={{0,2},{2,4},{4,6},{1,3},{3,5},{5,7},{8,10},{10,12},{12,14},{9,11},... | collective-permute-start | bytes 9224 | tf_op jit(solution)/shard_map/ppermute | solution.py:18
  127.8 0.8 collective-permute-done.9
  128.7 4.4 %collective-permute-start.11 = (f32[6,10,1]{2,1,0:T(8,128)S(1)}, f32[6,10,1]{2,1,0:T(8,128)S(1)}, u32[]{:S(2)}, u32[]{:S(2)}) collective-permute-start(f32[6,10,1]{2,1,0:T(8,128)S(1)} %get-tuple-element.111), channel_id=1, source_target_pairs={{0,1},{2,3},{4,5},{6,7},{8,9},{10,11},{12,13},{14,15},{16,17},{18,... | collective-permute-start | bytes 728 | tf_op jit(solution)/shard_map/ppermute | solution.py:18
  133.1 1.3 collective-permute-start.10
  134.4 0.1 scatter.26
  134.5 0.3 collective-permute-done.11
  134.8 4.5 %collective-permute-done.10 = f32[6,10,1]{2,1,0:T(8,128)S(1)} collective-permute-done((f32[6,10,1]{2,1,0:T(8,128)S(1)}, f32[6,10,1]{2,1,0:T(8,128)S(1)}, u32[]{:S(2)}, u32[]{:S(2)}) %collective-permute-start.10) | collective-permute-done | bytes 272 | tf_op jit(solution)/shard_map/ppermute | solution.py:19
  139.4 0.7 multiply_reduce_fusion.1
  140.1 0.5 convolution_bitcast_fusion.10
  140.5 41.6 %all-reduce.5 = (f32[22]{0:T(128)S(1)}, f32[]{:T(128)}) all-reduce(f32[22]{0:T(128)S(1)} %convolution_bitcast_fusion.10, f32[]{:T(128)} %get-tuple-element.102), channel_id=1, replica_groups=mesh['gx'=4,'gy'=4,'gz'=2] {'gx','gy','gz'}, use_global_device_ids=true, to_apply=%region_4.0 | all-reduce | flops 23 | bytes 184 | tf_op jit(solution)/shard_map/psum | solution.py:78
  182.1 0.7 multiply_reduce_fusion.4
  182.9 0.4 fusion.36
  183.2 0.4 fusion.35
  184.9 0.7 fusion.13
  186.3 0.1 fusion.9
  186.5 1.3 collective-permute-start.12
  187.8 4.5 %collective-permute-start.13 = (f32[1,8,128]{2,1,0:T(8,128)S(1)}, f32[1,8,128]{2,1,0:T(8,128)S(1)}, u32[]{:S(2)}, u32[]{:S(2)}) collective-permute-start(f32[1,8,128]{2,1,0:T(8,128)S(1)} %get-tuple-element.120), channel_id=1, source_target_pairs={{0,8},{8,16},{16,24},{1,9},{9,17},{17,25},{2,10},{10,18},{18,26},{... | collective-permute-start | bytes 12296 | tf_op jit(solution)/shard_map/ppermute | solution.py:18
  192.6 1.0 collective-permute-done.13
  193.7 1.3 collective-permute-start.14
  195.0 3.0 %collective-permute-start.15 = (f32[6,1,128]{2,1,0:T(1,128)S(1)}, f32[6,1,128]{2,1,0:T(1,128)S(1)}, u32[]{:S(2)}, u32[]{:S(2)}) collective-permute-start(f32[6,1,128]{2,1,0:T(1,128)S(1)} %get-tuple-element.114), channel_id=1, source_target_pairs={{0,2},{2,4},{4,6},{1,3},{3,5},{5,7},{8,10},{10,12},{12,14},{9,11},... | collective-permute-start | bytes 9224 | tf_op jit(solution)/shard_map/ppermute | solution.py:18
  198.0 0.8 collective-permute-done.15
  198.9 4.4 %collective-permute-start.17 = (f32[6,10,1]{2,1,0:T(8,128)S(1)}, f32[6,10,1]{2,1,0:T(8,128)S(1)}, u32[]{:S(2)}, u32[]{:S(2)}) collective-permute-start(f32[6,10,1]{2,1,0:T(8,128)S(1)} %get-tuple-element.109), channel_id=1, source_target_pairs={{0,1},{2,3},{4,5},{6,7},{8,9},{10,11},{12,13},{14,15},{16,17},{18,... | collective-permute-start | bytes 728 | tf_op jit(solution)/shard_map/ppermute | solution.py:18
  203.3 1.3 collective-permute-start.16
  204.6 0.1 scatter.30
  204.7 0.3 collective-permute-done.17
  205.0 4.5 %collective-permute-done.16 = f32[6,10,1]{2,1,0:T(8,128)S(1)} collective-permute-done((f32[6,10,1]{2,1,0:T(8,128)S(1)}, f32[6,10,1]{2,1,0:T(8,128)S(1)}, u32[]{:S(2)}, u32[]{:S(2)}) %collective-permute-start.16) | collective-permute-done | bytes 272 | tf_op jit(solution)/shard_map/ppermute | solution.py:19
  209.5 0.7 multiply_reduce_fusion
  210.2 0.5 convolution_bitcast_fusion.9
  210.7 41.6 %all-reduce.4 = (f32[23]{0:T(128)S(1)}, f32[]{:T(128)}) all-reduce(f32[23]{0:T(128)S(1)} %convolution_bitcast_fusion.9, f32[]{:T(128)} %get-tuple-element.98), channel_id=1, replica_groups=mesh['gx'=4,'gy'=4,'gz'=2] {'gx','gy','gz'}, use_global_device_ids=true, to_apply=%region_7.0 | all-reduce | flops 24 | bytes 192 | tf_op jit(solution)/shard_map/psum | solution.py:78
  252.3 0.7 multiply_reduce_fusion.3
  253.0 0.8 fusion.14
  253.8 0.4 fusion.38
  254.2 0.4 fusion.37
  256.5 0.2 concatenate.183
  256.8 0.8 copy.15
  257.7 0.6 pad_maximum_fusion.77
  (44 shorter events, 1.3 us)
Async XLA Ops:
  0.6 1.2 copy-start
  0.6 3.1 %copy-start.3 = (f32[4,8,128]{2,1,0:T(8,128)S(1)}, f32[4,8,128]{2,1,0:T(8,128)}, u32[]{:S(2)}) copy-start(f32[4,8,128]{2,1,0:T(8,128)} %param.21) | copy-start | bytes 49156
  47.6 6.1 %collective-permute-start = (f32[1,8,128]{2,1,0:T(8,128)S(1)}, f32[1,8,128]{2,1,0:T(8,128)S(1)}, u32[]{:S(2)}, u32[]{:S(2)}) collective-permute-start(f32[1,8,128]{2,1,0:T(8,128)S(1)} %get-tuple-element.125), channel_id=1, source_target_pairs={{8,0},{16,8},{24,16},{9,1},{17,9},{25,17},{10,2},{18,10},{26,18},{... | collective-permute-start | bytes 12296 | tf_op jit(solution)/shard_map/ppermute | solution.py:19
  48.9 5.9 %collective-permute-start.1 = (f32[1,8,128]{2,1,0:T(8,128)S(1)}, f32[1,8,128]{2,1,0:T(8,128)S(1)}, u32[]{:S(2)}, u32[]{:S(2)}) collective-permute-start(f32[1,8,128]{2,1,0:T(8,128)S(1)} %get-tuple-element.124), channel_id=1, source_target_pairs={{0,8},{8,16},{16,24},{1,9},{9,17},{17,25},{2,10},{10,18},{18,26},{... | collective-permute-start | bytes 12296 | tf_op jit(solution)/shard_map/ppermute | solution.py:18
  54.8 4.5 %collective-permute-start.2 = (f32[6,1,128]{2,1,0:T(1,128)S(1)}, f32[6,1,128]{2,1,0:T(1,128)S(1)}, u32[]{:S(2)}, u32[]{:S(2)}) collective-permute-start(f32[6,1,128]{2,1,0:T(1,128)S(1)} %get-tuple-element.119), channel_id=1, source_target_pairs={{2,0},{4,2},{6,4},{3,1},{5,3},{7,5},{10,8},{12,10},{14,12},{11,9},... | collective-permute-start | bytes 9224 | tf_op jit(solution)/shard_map/ppermute | solution.py:19
  56.1 3.8 %collective-permute-start.3 = (f32[6,1,128]{2,1,0:T(1,128)S(1)}, f32[6,1,128]{2,1,0:T(1,128)S(1)}, u32[]{:S(2)}, u32[]{:S(2)}) collective-permute-start(f32[6,1,128]{2,1,0:T(1,128)S(1)} %get-tuple-element.118), channel_id=1, source_target_pairs={{0,2},{2,4},{4,6},{1,3},{3,5},{5,7},{8,10},{10,12},{12,14},{9,11},... | collective-permute-start | bytes 9224 | tf_op jit(solution)/shard_map/ppermute | solution.py:18
  60.0 5.9 %collective-permute-start.5 = (f32[6,10,1]{2,1,0:T(8,128)S(1)}, f32[6,10,1]{2,1,0:T(8,128)S(1)}, u32[]{:S(2)}, u32[]{:S(2)}) collective-permute-start(f32[6,10,1]{2,1,0:T(8,128)S(1)} %get-tuple-element.113), channel_id=1, source_target_pairs={{0,1},{2,3},{4,5},{6,7},{8,9},{10,11},{12,13},{14,15},{16,17},{18,... | collective-permute-start | bytes 728 | tf_op jit(solution)/shard_map/ppermute | solution.py:18
  64.2 6.0 %collective-permute-start.4 = (f32[6,10,1]{2,1,0:T(8,128)S(1)}, f32[6,10,1]{2,1,0:T(8,128)S(1)}, u32[]{:S(2)}, u32[]{:S(2)}) collective-permute-start(f32[6,10,1]{2,1,0:T(8,128)S(1)} %get-tuple-element.112), channel_id=1, source_target_pairs={{1,0},{3,2},{5,4},{7,6},{9,8},{11,10},{13,12},{15,14},{17,16},{19,... | collective-permute-start | bytes 728 | tf_op jit(solution)/shard_map/ppermute | solution.py:19
  65.6 4.6 %copy-start.1 = (f32[3,4,8,128]{3,2,1,0:T(8,128)S(1)}, f32[3,4,8,128]{3,2,1,0:T(8,128)}, u32[]{:S(2)}) copy-start(f32[3,4,8,128]{3,2,1,0:T(8,128)} %param.23) | copy-start | bytes 147460
  65.6 4.6 %copy-start.2 = (f32[4,8,128]{2,1,0:T(8,128)S(1)}, f32[4,8,128]{2,1,0:T(8,128)}, u32[]{:S(2)}) copy-start(f32[4,8,128]{2,1,0:T(8,128)} %param.22) | copy-start | bytes 49156
  116.3 6.2 %collective-permute-start.6 = (f32[1,8,128]{2,1,0:T(8,128)S(1)}, f32[1,8,128]{2,1,0:T(8,128)S(1)}, u32[]{:S(2)}, u32[]{:S(2)}) collective-permute-start(f32[1,8,128]{2,1,0:T(8,128)S(1)} %get-tuple-element.123), channel_id=1, source_target_pairs={{8,0},{16,8},{24,16},{9,1},{17,9},{25,17},{10,2},{18,10},{26,18},{... | collective-permute-start | bytes 12296 | tf_op jit(solution)/shard_map/ppermute | solution.py:19
  117.6 5.9 %collective-permute-start.7 = (f32[1,8,128]{2,1,0:T(8,128)S(1)}, f32[1,8,128]{2,1,0:T(8,128)S(1)}, u32[]{:S(2)}, u32[]{:S(2)}) collective-permute-start(f32[1,8,128]{2,1,0:T(8,128)S(1)} %get-tuple-element.122), channel_id=1, source_target_pairs={{0,8},{8,16},{16,24},{1,9},{9,17},{17,25},{2,10},{10,18},{18,26},{... | collective-permute-start | bytes 12296 | tf_op jit(solution)/shard_map/ppermute | solution.py:18
  123.5 4.3 %collective-permute-start.8 = (f32[6,1,128]{2,1,0:T(1,128)S(1)}, f32[6,1,128]{2,1,0:T(1,128)S(1)}, u32[]{:S(2)}, u32[]{:S(2)}) collective-permute-start(f32[6,1,128]{2,1,0:T(1,128)S(1)} %get-tuple-element.117), channel_id=1, source_target_pairs={{2,0},{4,2},{6,4},{3,1},{5,3},{7,5},{10,8},{12,10},{14,12},{11,9},... | collective-permute-start | bytes 9224 | tf_op jit(solution)/shard_map/ppermute | solution.py:19
  124.8 3.8 %collective-permute-start.9 = (f32[6,1,128]{2,1,0:T(1,128)S(1)}, f32[6,1,128]{2,1,0:T(1,128)S(1)}, u32[]{:S(2)}, u32[]{:S(2)}) collective-permute-start(f32[6,1,128]{2,1,0:T(1,128)S(1)} %get-tuple-element.116), channel_id=1, source_target_pairs={{0,2},{2,4},{4,6},{1,3},{3,5},{5,7},{8,10},{10,12},{12,14},{9,11},... | collective-permute-start | bytes 9224 | tf_op jit(solution)/shard_map/ppermute | solution.py:18
  128.7 6.1 %collective-permute-start.11 = (f32[6,10,1]{2,1,0:T(8,128)S(1)}, f32[6,10,1]{2,1,0:T(8,128)S(1)}, u32[]{:S(2)}, u32[]{:S(2)}) collective-permute-start(f32[6,10,1]{2,1,0:T(8,128)S(1)} %get-tuple-element.111), channel_id=1, source_target_pairs={{0,1},{2,3},{4,5},{6,7},{8,9},{10,11},{12,13},{14,15},{16,17},{18,... | collective-permute-start | bytes 728 | tf_op jit(solution)/shard_map/ppermute | solution.py:18
  133.1 6.3 %collective-permute-start.10 = (f32[6,10,1]{2,1,0:T(8,128)S(1)}, f32[6,10,1]{2,1,0:T(8,128)S(1)}, u32[]{:S(2)}, u32[]{:S(2)}) collective-permute-start(f32[6,10,1]{2,1,0:T(8,128)S(1)} %get-tuple-element.110), channel_id=1, source_target_pairs={{1,0},{3,2},{5,4},{7,6},{9,8},{11,10},{13,12},{15,14},{17,16},{19,... | collective-permute-start | bytes 728 | tf_op jit(solution)/shard_map/ppermute | solution.py:19
  186.5 6.2 %collective-permute-start.12 = (f32[1,8,128]{2,1,0:T(8,128)S(1)}, f32[1,8,128]{2,1,0:T(8,128)S(1)}, u32[]{:S(2)}, u32[]{:S(2)}) collective-permute-start(f32[1,8,128]{2,1,0:T(8,128)S(1)} %get-tuple-element.121), channel_id=1, source_target_pairs={{8,0},{16,8},{24,16},{9,1},{17,9},{25,17},{10,2},{18,10},{26,18},{... | collective-permute-start | bytes 12296 | tf_op jit(solution)/shard_map/ppermute | solution.py:19
  187.8 5.9 %collective-permute-start.13 = (f32[1,8,128]{2,1,0:T(8,128)S(1)}, f32[1,8,128]{2,1,0:T(8,128)S(1)}, u32[]{:S(2)}, u32[]{:S(2)}) collective-permute-start(f32[1,8,128]{2,1,0:T(8,128)S(1)} %get-tuple-element.120), channel_id=1, source_target_pairs={{0,8},{8,16},{16,24},{1,9},{9,17},{17,25},{2,10},{10,18},{18,26},{... | collective-permute-start | bytes 12296 | tf_op jit(solution)/shard_map/ppermute | solution.py:18
  193.7 4.3 %collective-permute-start.14 = (f32[6,1,128]{2,1,0:T(1,128)S(1)}, f32[6,1,128]{2,1,0:T(1,128)S(1)}, u32[]{:S(2)}, u32[]{:S(2)}) collective-permute-start(f32[6,1,128]{2,1,0:T(1,128)S(1)} %get-tuple-element.115), channel_id=1, source_target_pairs={{2,0},{4,2},{6,4},{3,1},{5,3},{7,5},{10,8},{12,10},{14,12},{11,9},... | collective-permute-start | bytes 9224 | tf_op jit(solution)/shard_map/ppermute | solution.py:19
  195.0 3.8 %collective-permute-start.15 = (f32[6,1,128]{2,1,0:T(1,128)S(1)}, f32[6,1,128]{2,1,0:T(1,128)S(1)}, u32[]{:S(2)}, u32[]{:S(2)}) collective-permute-start(f32[6,1,128]{2,1,0:T(1,128)S(1)} %get-tuple-element.114), channel_id=1, source_target_pairs={{0,2},{2,4},{4,6},{1,3},{3,5},{5,7},{8,10},{10,12},{12,14},{9,11},... | collective-permute-start | bytes 9224 | tf_op jit(solution)/shard_map/ppermute | solution.py:18
  198.9 6.1 %collective-permute-start.17 = (f32[6,10,1]{2,1,0:T(8,128)S(1)}, f32[6,10,1]{2,1,0:T(8,128)S(1)}, u32[]{:S(2)}, u32[]{:S(2)}) collective-permute-start(f32[6,10,1]{2,1,0:T(8,128)S(1)} %get-tuple-element.109), channel_id=1, source_target_pairs={{0,1},{2,3},{4,5},{6,7},{8,9},{10,11},{12,13},{14,15},{16,17},{18,... | collective-permute-start | bytes 728 | tf_op jit(solution)/shard_map/ppermute | solution.py:18
  203.3 6.3 %collective-permute-start.16 = (f32[6,10,1]{2,1,0:T(8,128)S(1)}, f32[6,10,1]{2,1,0:T(8,128)S(1)}, u32[]{:S(2)}, u32[]{:S(2)}) collective-permute-start(f32[6,10,1]{2,1,0:T(8,128)S(1)} %get-tuple-element.108), channel_id=1, source_target_pairs={{1,0},{3,2},{5,4},{7,6},{9,8},{11,10},{13,12},{15,14},{17,16},{19,... | collective-permute-start | bytes 728 | tf_op jit(solution)/shard_map/ppermute | solution.py:19
where the time goes:
time: 260 us; the launch traced here: 258 us
  blocking collectives  166 us (64%)
  starting transfers between devices  47.2 us (18%)
  waiting for transfers between devices  19.5 us (8%)
  matrix products  10.7 us (4%)
  between operations  7.79 us (3%)
  local copies, waits for them, and re-layouts  4 us (2%)
  other arithmetic  3.24 us (1%)
    psum x3, blocking collectives, per_device(): lax.psum((jnp.dot(flat_basis, applied, precision=highest), jnp.sum(applie...  124 us
    psum x1, blocking collectives, per_device(): lax.psum(jnp.dot(flat_start, flat_start.T, precision=highest), ('gx', 'gy...  42.1 us
    ppermute x9, starting transfers between devices, with_halo(): before = lax.ppermute(last, axis, up)  35.6 us
    ppermute x9, waiting for transfers between devices, with_halo(): after = lax.ppermute(initial, axis, down)  13.4 us
    ppermute x9, starting transfers between devices, with_halo(): after = lax.ppermute(initial, axis, down)  11.6 us
    ppermute x9, waiting for transfers between devices, with_halo(): before = lax.ppermute(last, axis, up)  6.12 us
  transfers between devices with their start and end apart: 18, of which 12 were waited for; matrix products, arithmetic and copies ran while one was open for 0% of the time, Pallas kernels for 0%

commit v1 on v0

--- a/solution.py
+++ b/solution.py
@@ -64,7 +64,12 @@
     starting = jnp.concatenate([rotated, next_vector[None]], axis=0)
     flat_start = starting.reshape(KEEP + 1, -1)
     gram_matrix = (
-        lax.psum(jnp.dot(flat_start, flat_start.T, precision=highest), ("gx", "gy", "gz"))
+        jnp.sum(
+            lax.all_gather(
+                jnp.dot(flat_start, flat_start.T, precision=highest), ("gx", "gy", "gz")
+            ),
+            axis=0,
+        )
         / cell_count
     )
     divisor = jnp.maximum(jnp.sqrt(gram_matrix[KEEP, KEEP]), 0.5)

time: 260 us -> 284 us (1.092)
  blocking collectives: 166 us -> 192 us
  starting transfers between devices: 47.2 us -> 37.7 us
  waiting for transfers between devices: 19.5 us -> 27 us
    all_gather x0 -> x1, blocking collectives: none -> 71.8 us  [per_device(): lax.all_gather(jnp.dot(flat_start, flat_start.T, precision=highest), ('gx...]
    psum x1 -> x0, blocking collectives: 42.1 us -> none  [per_device(): lax.psum(jnp.dot(flat_start, flat_start.T, precision=highest), ('gx', 'gy...]
    ppermute x9, starting transfers between devices: 35.6 us -> 26 us  [with_halo(): before = lax.ppermute(last, axis, up)]
    ppermute x9, waiting for transfers between devices: 13.4 us -> 22.4 us  [with_halo(): after = lax.ppermute(initial, axis, down)]
    psum x3, blocking collectives: 124 us -> 120 us  [per_device(): lax.psum((jnp.dot(flat_basis, applied, precision=highest), jnp.sum(applie...]
  transfers between devices with their start and end apart: 18 -> 18, of which waited for: 12 -> 9; matrix products, arithmetic and copies ran while one was open for 0% -> 0% of each run, Pallas kernels for 0% -> 0%
where the time goes in v1:
time: 284 us; the launch traced here: 283 us
  blocking collectives  192 us (68%)
  starting transfers between devices  37.7 us (13%)
  waiting for transfers between devices  27 us (10%)
  matrix products  10.7 us (4%)
  between operations  7.79 us (3%)
  local copies, waits for them, and re-layouts  4.01 us (1%)
  other arithmetic  3.28 us (1%)
    psum x3, blocking collectives, per_device(): lax.psum((jnp.dot(flat_basis, applied, precision=highest), jnp.sum(applie...  120 us
    all_gather x1, blocking collectives, per_device(): lax.all_gather(jnp.dot(flat_start, flat_start.T, precision=highest), ('gx...  71.8 us
    ppermute x9, starting transfers between devices, with_halo(): before = lax.ppermute(last, axis, up)  26 us
    ppermute x9, waiting for transfers between devices, with_halo(): after = lax.ppermute(initial, axis, down)  22.4 us
    ppermute x9, starting transfers between devices, with_halo(): after = lax.ppermute(initial, axis, down)  11.6 us
  transfers between devices with their start and end apart: 18, of which 9 were waited for; matrix products, arithmetic and copies ran while one was open for 0% of the time, Pallas kernels for 0%

profile of v1, /device:TPU:0, one launch (start us, length us, event | category | flops | bytes accessed | tf_op | source)
XLA Modules:
  0.0 282.6 jit_solution(16688121294808265239)
XLA Ops:
  0.7 1.2 copy-done
  1.8 1.9 fusion.10
  3.7 0.5 convolution_bitcast_fusion
  4.2 71.8 %all-gather.1 = f32[32,21,21]{2,1,0:T(8,128)S(1)} all-gather(f32[1,21,21]{2,1,0:T(8,128)S(1)} %convolution_bitcast_fusion), channel_id=2, replica_groups=mesh['gx'=4,'gy'=4,'gz'=2] {'gx','gy','gz'}, dimensions={0}, use_global_device_ids=true | all-gather | bytes 58212 | tf_op jit(solution)/shard_map/all_gather | solution.py:68
  76.1 0.6 slice.304
  77.4 1.3 collective-permute-start.1
  78.7 1.3 collective-permute-start
  80.2 4.0 %collective-permute-done = f32[1,8,128]{2,1,0:T(8,128)S(1)} collective-permute-done((f32[1,8,128]{2,1,0:T(8,128)S(1)}, f32[1,8,128]{2,1,0:T(8,128)S(1)}, u32[]{:S(2)}, u32[]{:S(2)}) %collective-permute-start) | collective-permute-done | bytes 4128 | tf_op jit(solution)/shard_map/ppermute | solution.py:19
  84.2 1.3 collective-permute-start.3
  85.4 1.3 collective-permute-start.2
  86.9 1.6 collective-permute-done.2
  88.6 1.3 collective-permute-start.4
  89.9 4.5 %collective-permute-start.5 = (f32[6,10,1]{2,1,0:T(8,128)S(1)}, f32[6,10,1]{2,1,0:T(8,128)S(1)}, u32[]{:S(2)}, u32[]{:S(2)}) collective-permute-start(f32[6,10,1]{2,1,0:T(8,128)S(1)} %get-tuple-element.115), channel_id=1, source_target_pairs={{0,1},{2,3},{4,5},{6,7},{8,9},{10,11},{12,13},{14,15},{16,17},{18,... | collective-permute-start | bytes 728 | tf_op jit(solution)/shard_map/ppermute | solution.py:18
  94.5 0.2 copy.41
  94.8 1.4 collective-permute-done.5
  96.2 0.7 multiply_reduce_fusion.2
  96.9 0.5 convolution_bitcast_fusion.11
  97.4 38.0 %all-reduce.6 = (f32[21]{0:T(128)S(1)}, f32[]{:T(128)}) all-reduce(f32[21]{0:T(128)S(1)} %convolution_bitcast_fusion.11, f32[]{:T(128)} %get-tuple-element.108), channel_id=1, replica_groups=mesh['gx'=4,'gy'=4,'gz'=2] {'gx','gy','gz'}, use_global_device_ids=true, to_apply=%region_1.0 | all-reduce | flops 22 | bytes 176 | tf_op jit(solution)/shard_map/psum | solution.py:83
  136.1 0.7 multiply_reduce_fusion.5
  136.8 0.7 fusion.12
  138.9 0.1 fusion.8
  139.0 0.3 fusion.33
  139.4 0.3 fusion.34
  139.8 0.1 copy.18
  139.9 4.1 %collective-permute-start.7 = (f32[1,8,128]{2,1,0:T(8,128)S(1)}, f32[1,8,128]{2,1,0:T(8,128)S(1)}, u32[]{:S(2)}, u32[]{:S(2)}) collective-permute-start(f32[1,8,128]{2,1,0:T(8,128)S(1)} %get-tuple-element.124), channel_id=1, source_target_pairs={{0,8},{8,16},{16,24},{1,9},{9,17},{17,25},{2,10},{10,18},{18,26},{... | collective-permute-start | bytes 12296 | tf_op jit(solution)/shard_map/ppermute | solution.py:18
  144.1 1.3 collective-permute-start.6
  145.4 4.1 %collective-permute-done.6 = f32[1,8,128]{2,1,0:T(8,128)S(1)} collective-permute-done((f32[1,8,128]{2,1,0:T(8,128)S(1)}, f32[1,8,128]{2,1,0:T(8,128)S(1)}, u32[]{:S(2)}, u32[]{:S(2)}) %collective-permute-start.6) | collective-permute-done | bytes 4128 | tf_op jit(solution)/shard_map/ppermute | solution.py:19
  149.6 1.3 collective-permute-start.9
  150.9 1.3 collective-permute-start.8
  152.2 4.2 %collective-permute-done.8 = f32[6,1,128]{2,1,0:T(1,128)S(1)} collective-permute-done((f32[6,1,128]{2,1,0:T(1,128)S(1)}, f32[6,1,128]{2,1,0:T(1,128)S(1)}, u32[]{:S(2)}, u32[]{:S(2)}) %collective-permute-start.8) | collective-permute-done | bytes 3104 | tf_op jit(solution)/shard_map/ppermute | solution.py:19
  156.5 1.3 collective-permute-start.10
  157.8 4.5 %collective-permute-start.11 = (f32[6,10,1]{2,1,0:T(8,128)S(1)}, f32[6,10,1]{2,1,0:T(8,128)S(1)}, u32[]{:S(2)}, u32[]{:S(2)}) collective-permute-start(f32[6,10,1]{2,1,0:T(8,128)S(1)} %get-tuple-element.113), channel_id=1, source_target_pairs={{0,1},{2,3},{4,5},{6,7},{8,9},{10,11},{12,13},{14,15},{16,17},{18,... | collective-permute-start | bytes 728 | tf_op jit(solution)/shard_map/ppermute | solution.py:18
  162.4 0.1 scatter.26
  162.5 1.6 collective-permute-done.11
  164.1 0.7 multiply_reduce_fusion.1
  164.8 0.5 convolution_bitcast_fusion.10
  165.3 41.2 %all-reduce.5 = (f32[22]{0:T(128)S(1)}, f32[]{:T(128)}) all-reduce(f32[22]{0:T(128)S(1)} %convolution_bitcast_fusion.10, f32[]{:T(128)} %get-tuple-element.104), channel_id=1, replica_groups=mesh['gx'=4,'gy'=4,'gz'=2] {'gx','gy','gz'}, use_global_device_ids=true, to_apply=%region_4.0 | all-reduce | flops 23 | bytes 184 | tf_op jit(solution)/shard_map/psum | solution.py:83
  207.2 0.7 multiply_reduce_fusion.4
  208.6 0.7 fusion.13
  210.0 0.1 fusion.9
  210.1 0.4 fusion.35
  210.5 0.4 fusion.36
  211.0 0.1 copy.19
  211.1 3.2 %collective-permute-start.13 = (f32[1,8,128]{2,1,0:T(8,128)S(1)}, f32[1,8,128]{2,1,0:T(8,128)S(1)}, u32[]{:S(2)}, u32[]{:S(2)}) collective-permute-start(f32[1,8,128]{2,1,0:T(8,128)S(1)} %get-tuple-element.122), channel_id=1, source_target_pairs={{0,8},{8,16},{16,24},{1,9},{9,17},{17,25},{2,10},{10,18},{18,26},{... | collective-permute-start | bytes 12296 | tf_op jit(solution)/shard_map/ppermute | solution.py:18
  214.3 1.3 collective-permute-start.12
  215.7 4.1 %collective-permute-done.12 = f32[1,8,128]{2,1,0:T(8,128)S(1)} collective-permute-done((f32[1,8,128]{2,1,0:T(8,128)S(1)}, f32[1,8,128]{2,1,0:T(8,128)S(1)}, u32[]{:S(2)}, u32[]{:S(2)}) %collective-permute-start.12) | collective-permute-done | bytes 4128 | tf_op jit(solution)/shard_map/ppermute | solution.py:19
  219.8 1.3 collective-permute-start.15
  221.1 1.3 collective-permute-start.14
  222.4 4.2 %collective-permute-done.14 = f32[6,1,128]{2,1,0:T(1,128)S(1)} collective-permute-done((f32[6,1,128]{2,1,0:T(1,128)S(1)}, f32[6,1,128]{2,1,0:T(1,128)S(1)}, u32[]{:S(2)}, u32[]{:S(2)}) %collective-permute-start.14) | collective-permute-done | bytes 3104 | tf_op jit(solution)/shard_map/ppermute | solution.py:19
  226.7 1.3 collective-permute-start.16
  228.0 4.5 %collective-permute-start.17 = (f32[6,10,1]{2,1,0:T(8,128)S(1)}, f32[6,10,1]{2,1,0:T(8,128)S(1)}, u32[]{:S(2)}, u32[]{:S(2)}) collective-permute-start(f32[6,10,1]{2,1,0:T(8,128)S(1)} %get-tuple-element.111), channel_id=1, source_target_pairs={{0,1},{2,3},{4,5},{6,7},{8,9},{10,11},{12,13},{14,15},{16,17},{18,... | collective-permute-start | bytes 728 | tf_op jit(solution)/shard_map/ppermute | solution.py:18
  232.6 0.1 scatter.30
  232.7 1.6 collective-permute-done.17
  234.3 0.7 multiply_reduce_fusion
  235.0 0.5 convolution_bitcast_fusion.9
  235.5 41.1 %all-reduce.4 = (f32[23]{0:T(128)S(1)}, f32[]{:T(128)}) all-reduce(f32[23]{0:T(128)S(1)} %convolution_bitcast_fusion.9, f32[]{:T(128)} %get-tuple-element.100), channel_id=1, replica_groups=mesh['gx'=4,'gy'=4,'gz'=2] {'gx','gy','gz'}, use_global_device_ids=true, to_apply=%region_7.0 | all-reduce | flops 24 | bytes 192 | tf_op jit(solution)/shard_map/psum | solution.py:83
  276.6 0.7 multiply_reduce_fusion.3
  277.4 0.8 fusion.14
  280.1 0.4 fusion.38
  280.5 0.4 fusion.37
  280.9 0.2 concatenate.183
  281.1 0.8 copy.20
  281.9 0.1 scatter.34
  282.0 0.6 pad_maximum_fusion.77
  (45 shorter events, 1.1 us)
Async XLA Ops:
  0.6 1.2 copy-start
  0.6 3.1 %copy-start.3 = (f32[4,8,128]{2,1,0:T(8,128)S(1)}, f32[4,8,128]{2,1,0:T(8,128)}, u32[]{:S(2)}) copy-start(f32[4,8,128]{2,1,0:T(8,128)} %param.21) | copy-start | bytes 49156
  77.4 2.8 collective-permute-start.1
  78.7 5.5 %collective-permute-start = (f32[1,8,128]{2,1,0:T(8,128)S(1)}, f32[1,8,128]{2,1,0:T(8,128)S(1)}, u32[]{:S(2)}, u32[]{:S(2)}) collective-permute-start(f32[1,8,128]{2,1,0:T(8,128)S(1)} %get-tuple-element.127), channel_id=1, source_target_pairs={{8,0},{16,8},{24,16},{9,1},{17,9},{25,17},{10,2},{18,10},{26,18},{... | collective-permute-start | bytes 12296 | tf_op jit(solution)/shard_map/ppermute | solution.py:19
  84.2 2.7 collective-permute-start.3
  85.4 3.1 %collective-permute-start.2 = (f32[6,1,128]{2,1,0:T(1,128)S(1)}, f32[6,1,128]{2,1,0:T(1,128)S(1)}, u32[]{:S(2)}, u32[]{:S(2)}) collective-permute-start(f32[6,1,128]{2,1,0:T(1,128)S(1)} %get-tuple-element.121), channel_id=1, source_target_pairs={{2,0},{4,2},{6,4},{3,1},{5,3},{7,5},{10,8},{12,10},{14,12},{11,9},... | collective-permute-start | bytes 9224 | tf_op jit(solution)/shard_map/ppermute | solution.py:19
  88.6 6.2 %collective-permute-start.4 = (f32[6,10,1]{2,1,0:T(8,128)S(1)}, f32[6,10,1]{2,1,0:T(8,128)S(1)}, u32[]{:S(2)}, u32[]{:S(2)}) collective-permute-start(f32[6,10,1]{2,1,0:T(8,128)S(1)} %get-tuple-element.114), channel_id=1, source_target_pairs={{1,0},{3,2},{5,4},{7,6},{9,8},{11,10},{13,12},{15,14},{17,16},{19,... | collective-permute-start | bytes 728 | tf_op jit(solution)/shard_map/ppermute | solution.py:19
  89.9 6.3 %collective-permute-start.5 = (f32[6,10,1]{2,1,0:T(8,128)S(1)}, f32[6,10,1]{2,1,0:T(8,128)S(1)}, u32[]{:S(2)}, u32[]{:S(2)}) collective-permute-start(f32[6,10,1]{2,1,0:T(8,128)S(1)} %get-tuple-element.115), channel_id=1, source_target_pairs={{0,1},{2,3},{4,5},{6,7},{8,9},{10,11},{12,13},{14,15},{16,17},{18,... | collective-permute-start | bytes 728 | tf_op jit(solution)/shard_map/ppermute | solution.py:18
  94.5 1.7 copy-start.1
  94.5 1.7 copy-start.2
  139.9 5.5 %collective-permute-start.7 = (f32[1,8,128]{2,1,0:T(8,128)S(1)}, f32[1,8,128]{2,1,0:T(8,128)S(1)}, u32[]{:S(2)}, u32[]{:S(2)}) collective-permute-start(f32[1,8,128]{2,1,0:T(8,128)S(1)} %get-tuple-element.124), channel_id=1, source_target_pairs={{0,8},{8,16},{16,24},{1,9},{9,17},{17,25},{2,10},{10,18},{18,26},{... | collective-permute-start | bytes 12296 | tf_op jit(solution)/shard_map/ppermute | solution.py:18
  144.1 5.5 %collective-permute-start.6 = (f32[1,8,128]{2,1,0:T(8,128)S(1)}, f32[1,8,128]{2,1,0:T(8,128)S(1)}, u32[]{:S(2)}, u32[]{:S(2)}) collective-permute-start(f32[1,8,128]{2,1,0:T(8,128)S(1)} %get-tuple-element.125), channel_id=1, source_target_pairs={{8,0},{16,8},{24,16},{9,1},{17,9},{25,17},{10,2},{18,10},{26,18},{... | collective-permute-start | bytes 12296 | tf_op jit(solution)/shard_map/ppermute | solution.py:19
  149.6 2.6 collective-permute-start.9
  150.9 5.6 %collective-permute-start.8 = (f32[6,1,128]{2,1,0:T(1,128)S(1)}, f32[6,1,128]{2,1,0:T(1,128)S(1)}, u32[]{:S(2)}, u32[]{:S(2)}) collective-permute-start(f32[6,1,128]{2,1,0:T(1,128)S(1)} %get-tuple-element.119), channel_id=1, source_target_pairs={{2,0},{4,2},{6,4},{3,1},{5,3},{7,5},{10,8},{12,10},{14,12},{11,9},... | collective-permute-start | bytes 9224 | tf_op jit(solution)/shard_map/ppermute | solution.py:19
  156.5 6.0 %collective-permute-start.10 = (f32[6,10,1]{2,1,0:T(8,128)S(1)}, f32[6,10,1]{2,1,0:T(8,128)S(1)}, u32[]{:S(2)}, u32[]{:S(2)}) collective-permute-start(f32[6,10,1]{2,1,0:T(8,128)S(1)} %get-tuple-element.112), channel_id=1, source_target_pairs={{1,0},{3,2},{5,4},{7,6},{9,8},{11,10},{13,12},{15,14},{17,16},{19,... | collective-permute-start | bytes 728 | tf_op jit(solution)/shard_map/ppermute | solution.py:19
  157.8 6.3 %collective-permute-start.11 = (f32[6,10,1]{2,1,0:T(8,128)S(1)}, f32[6,10,1]{2,1,0:T(8,128)S(1)}, u32[]{:S(2)}, u32[]{:S(2)}) collective-permute-start(f32[6,10,1]{2,1,0:T(8,128)S(1)} %get-tuple-element.113), channel_id=1, source_target_pairs={{0,1},{2,3},{4,5},{6,7},{8,9},{10,11},{12,13},{14,15},{16,17},{18,... | collective-permute-start | bytes 728 | tf_op jit(solution)/shard_map/ppermute | solution.py:18
  211.1 4.6 %collective-permute-start.13 = (f32[1,8,128]{2,1,0:T(8,128)S(1)}, f32[1,8,128]{2,1,0:T(8,128)S(1)}, u32[]{:S(2)}, u32[]{:S(2)}) collective-permute-start(f32[1,8,128]{2,1,0:T(8,128)S(1)} %get-tuple-element.122), channel_id=1, source_target_pairs={{0,8},{8,16},{16,24},{1,9},{9,17},{17,25},{2,10},{10,18},{18,26},{... | collective-permute-start | bytes 12296 | tf_op jit(solution)/shard_map/ppermute | solution.py:18
  214.3 5.5 %collective-permute-start.12 = (f32[1,8,128]{2,1,0:T(8,128)S(1)}, f32[1,8,128]{2,1,0:T(8,128)S(1)}, u32[]{:S(2)}, u32[]{:S(2)}) collective-permute-start(f32[1,8,128]{2,1,0:T(8,128)S(1)} %get-tuple-element.123), channel_id=1, source_target_pairs={{8,0},{16,8},{24,16},{9,1},{17,9},{25,17},{10,2},{18,10},{26,18},{... | collective-permute-start | bytes 12296 | tf_op jit(solution)/shard_map/ppermute | solution.py:19
  219.8 2.6 collective-permute-start.15
  221.1 5.6 %collective-permute-start.14 = (f32[6,1,128]{2,1,0:T(1,128)S(1)}, f32[6,1,128]{2,1,0:T(1,128)S(1)}, u32[]{:S(2)}, u32[]{:S(2)}) collective-permute-start(f32[6,1,128]{2,1,0:T(1,128)S(1)} %get-tuple-element.117), channel_id=1, source_target_pairs={{2,0},{4,2},{6,4},{3,1},{5,3},{7,5},{10,8},{12,10},{14,12},{11,9},... | collective-permute-start | bytes 9224 | tf_op jit(solution)/shard_map/ppermute | solution.py:19
  226.7 6.0 %collective-permute-start.16 = (f32[6,10,1]{2,1,0:T(8,128)S(1)}, f32[6,10,1]{2,1,0:T(8,128)S(1)}, u32[]{:S(2)}, u32[]{:S(2)}) collective-permute-start(f32[6,10,1]{2,1,0:T(8,128)S(1)} %get-tuple-element.110), channel_id=1, source_target_pairs={{1,0},{3,2},{5,4},{7,6},{9,8},{11,10},{13,12},{15,14},{17,16},{19,... | collective-permute-start | bytes 728 | tf_op jit(solution)/shard_map/ppermute | solution.py:19
  228.0 6.3 %collective-permute-start.17 = (f32[6,10,1]{2,1,0:T(8,128)S(1)}, f32[6,10,1]{2,1,0:T(8,128)S(1)}, u32[]{:S(2)}, u32[]{:S(2)}) collective-permute-start(f32[6,10,1]{2,1,0:T(8,128)S(1)} %get-tuple-element.111), channel_id=1, source_target_pairs={{0,1},{2,3},{4,5},{6,7},{8,9},{10,11},{12,13},{14,15},{16,17},{18,... | collective-permute-start | bytes 728 | tf_op jit(solution)/shard_map/ppermute | solution.py:18
